TPU v7x, 32 devices: a whole 2x2x4 slice. The times are simulated.
32 devices in a mesh: dp: 2 (over y), seq: 4 (over x, core), tp: 4 (over z).
Axes of the slice: x: 2, y: 2, z: 4, core: 2. Of those that a mesh axis runs over, the one named last changes fastest.
Arguments:
- tokens: bfloat16 [2048, 4096], P(('dp', 'seq', 'tp')), parts along dimension 0, may hold values from -6 to 6
- pre_gain: float32 [4096], replicated, may hold values from 0.25 to 1.75
- proj_inner: bfloat16 [4096, 4096], P(None, 'tp'), may hold values from -0.09375 to 0.09375
- proj_gate: bfloat16 [4096, 4096], P(None, 'tp'), may hold values from -0.09375 to 0.09375
- proj_states: bfloat16 [4096, 1024], P(None, 'tp'), may hold values from -0.09375 to 0.09375
- proj_step: bfloat16 [4096, 64], P(None, 'tp'), may hold values from -0.09375 to 0.09375
- step_bias: float32 [64], P('tp'), may hold values from -5 to -3
- log_rate: float32 [64], P('tp'), as said below
- conv_inner: float32 [4, 4096], P(None, 'tp'), may hold values from -3 to 3
- conv_states: float32 [4, 1024], P(None, 'tp'), may hold values from -3 to 3
- skip_gain: float32 [64], P('tp'), may hold values from 1 to 4
- norm_gain: float32 [4096], P('tp'), may hold values from 0.25 to 1.75
- proj_output: bfloat16 [4096, 4096], P('tp'), may hold values from -0.09375 to 0.09375
Outputs:
- layer_out: bfloat16 [2048, 4096], P(('dp', 'seq', 'tp')), parts along dimension 0
There are 2 independent parts, one for each index of `dp`. A program takes and returns all parts, laid end to end along the dimension named above; an argument that names none is the same for every part. Nothing has to cross between parts.
Inputs may be any that keep to these rules, and one draw needn't show every extreme that they name: exp(log_rate) lies between 0.1 / (0.035 * 1024) and 1 / (25 * 0.035).
All inputs are finite; a program needn't handle non-finite values.
Results may differ from a plain program's by a relative error of at most 0.017.
Values may be sent and summed in bfloat16 or wider, within the bound.
A program may use at most 64 MiB of HBM per device.

v0:
```python
from functools import partial

import jax
import jax.numpy as jnp
from jax import lax
from jax.sharding import PartitionSpec as P
from jax.experimental import pallas as pl
from jax.experimental.pallas import tpu as pltpu

HEAD_DIM = 64
STATE = 128
GROUP_HEADS = 16
BLOCK = 128
GROUPS = 4


epsilon = 1e-05
highest = lax.Precision.HIGHEST


def from_behind(value, axis, steps):
    count = lax.axis_size(axis)
    initial, last = (max(0, -steps), min(count, count - steps))
    return lax.ppermute(value, axis, [(source, source + steps) for source in range(initial, last)])


def causal_conv(values, kernel_taps, before):
    length = values.shape[0]
    padded = jnp.concatenate((before, values), axis=0)
    running_sum = jnp.zeros(values.shape, jnp.float32)
    for offset in range(kernel_taps.shape[0]):
        running_sum = running_sum + kernel_taps[offset] * padded[offset : offset + length]
    return running_sum


def block_step(carry_state, inputs, copies):
    values, step_size, log_decay, in_states, out_states = inputs
    block_len = values.shape[0]
    running = jnp.cumsum(log_decay, axis=0)
    scores = jnp.einsum("tgn,sgn->gts", out_states, in_states, precision=highest)
    scores = jnp.tile(scores, (copies, 1, 1))
    places = jnp.arange(block_len)
    lower_mask = (places[:, None] >= places[None, :])[None]
    spread = running.T[:, :, None] - running.T[:, None, :]
    decay_table = jnp.where(lower_mask, jnp.exp(jnp.where(lower_mask, spread, 0.0)), 0.0)
    weights = scores * decay_table * step_size.T[:, None, :]
    within = jnp.einsum("hts,shp->thp", weights, values, precision=highest)
    out_heads = jnp.tile(out_states, (1, copies, 1))
    in_heads = jnp.tile(in_states, (1, copies, 1))
    carried = (
        jnp.einsum("thn,hpn->thp", out_heads, carry_state, precision=highest)
        * jnp.exp(running)[:, :, None]
    )
    tail_decay = jnp.exp(running[-1][None, :] - running) * step_size
    scaled = values * tail_decay[:, :, None]
    new_state = jnp.exp(running[-1])[:, None, None] * carry_state + jnp.einsum(
        "shp,shn->hpn", scaled, in_heads, precision=highest
    )
    return (new_state, within + carried)


def scan_blocks(
    values, step_size, log_decay, in_states, out_states, carry_state, block_len, copies
):
    row_count, head_count, head_dim = values.shape
    block_count = row_count // block_len

    def split_blocks(source):
        return source.reshape((block_count, block_len) + source.shape[1:])

    final_state, outputs = lax.scan(
        partial(block_step, copies=copies),
        carry_state,
        (
            split_blocks(values),
            split_blocks(step_size),
            split_blocks(log_decay),
            split_blocks(in_states),
            split_blocks(out_states),
        ),
    )
    return (final_state, outputs.reshape(row_count, head_count, head_dim))


def plain_body(
    tokens,
    pre_gain,
    proj_inner,
    proj_gate,
    proj_states,
    proj_step,
    step_bias,
    log_rate,
    conv_inner,
    conv_states,
    skip_gain,
    norm_gain,
    proj_output,
):
    tokens_wide = tokens.astype(jnp.float32)
    normed = (
        tokens_wide
        * lax.rsqrt(jnp.mean(tokens_wide * tokens_wide, axis=1, keepdims=True) + epsilon)
        * pre_gain
    ).astype(jnp.bfloat16)
    inner_width = proj_inner.shape[1]
    state_width = proj_states.shape[1]
    heads_local = proj_step.shape[1]
    copies = heads_local // GROUPS
    row_piece = lax.all_gather(normed, "tp", axis=0, tiled=True)
    projected = jnp.concatenate(
        (
            jnp.dot(row_piece, proj_inner, preferred_element_type=jnp.float32),
            jnp.dot(row_piece, proj_gate, preferred_element_type=jnp.float32),
            jnp.dot(row_piece, proj_states, preferred_element_type=jnp.float32),
            jnp.dot(row_piece, proj_step, preferred_element_type=jnp.float32),
        ),
        axis=1,
    )
    row_count = projected.shape[0]
    inner_proj = projected[:, :inner_width].astype(jnp.bfloat16)
    gate_proj = projected[:, inner_width : 2 * inner_width].astype(jnp.bfloat16)
    state_proj = projected[:, 2 * inner_width : 2 * inner_width + state_width].astype(jnp.bfloat16)
    step_size = jax.nn.softplus(projected[:, 2 * inner_width + state_width :] + step_bias)
    log_decay = -jnp.exp(log_rate) * step_size
    margin = conv_inner.shape[0] - 1
    before_inner, before_states = from_behind(
        (inner_proj[row_count - margin :], state_proj[row_count - margin :]), "seq", 1
    )
    mixed_inner = jax.nn.silu(
        causal_conv(inner_proj.astype(jnp.float32), conv_inner, before_inner.astype(jnp.float32))
    ).astype(jnp.bfloat16)
    mixed_local = jax.nn.silu(
        causal_conv(state_proj.astype(jnp.float32), conv_states, before_states.astype(jnp.float32))
    ).astype(jnp.bfloat16)
    mixed_all = lax.all_gather(mixed_local, "tp", axis=1, tiled=True)
    values = mixed_inner.astype(jnp.float32).reshape(row_count, heads_local, HEAD_DIM)
    paired = mixed_all.astype(jnp.float32).reshape(row_count, GROUPS, 2, STATE)
    in_states = paired[:, :, 0]
    out_states = paired[:, :, 1]
    zero_state = jnp.zeros((heads_local, HEAD_DIM, STATE), jnp.float32)
    final_state, scanned = scan_blocks(
        values, step_size, log_decay, in_states, out_states, zero_state, BLOCK, copies
    )
    decay_sum = jnp.sum(log_decay, axis=0)
    decay_sums, summaries = (
        lax.all_gather(decay_sum[None].astype(jnp.bfloat16), "seq", axis=0, tiled=True).astype(
            jnp.float32
        ),
        lax.all_gather(final_state[None].astype(jnp.bfloat16), "seq", axis=0, tiled=True).astype(
            jnp.float32
        ),
    )
    position = lax.axis_index("seq")
    device_ids = jnp.arange(decay_sums.shape[0])
    earlier_mask = (device_ids < position)[:, None]
    before_me = jnp.sum(jnp.where(earlier_mask, decay_sums, 0.0), axis=0)
    reach_end = jnp.cumsum(decay_sums, axis=0)
    weights = jnp.where(
        earlier_mask, jnp.exp(jnp.where(earlier_mask, before_me[None] - reach_end, 0.0)), 0.0
    )
    incoming = jnp.einsum("jh,jhpn->hpn", weights, summaries, precision=highest)
    running = jnp.cumsum(log_decay, axis=0)
    out_heads = jnp.tile(out_states, (1, copies, 1))
    carried = (
        jnp.einsum("thn,hpn->thp", out_heads, incoming, precision=highest)
        * jnp.exp(running)[:, :, None]
    )
    ssd_out = scanned + carried + skip_gain[None, :, None] * values
    gated_out = ssd_out * jax.nn.silu(gate_proj.astype(jnp.float32)).reshape(
        row_count, heads_local, HEAD_DIM
    )
    head_squares = jnp.sum(gated_out * gated_out, axis=2)
    every_square = lax.all_gather(head_squares, "tp", axis=1, tiled=True)
    group_totals = jnp.sum(
        every_square.reshape(row_count, every_square.shape[1] // GROUPS, GROUPS), axis=1
    )
    mean_square = (group_totals / (GROUP_HEADS * HEAD_DIM))[:, None, :, None]
    grouped = gated_out.reshape(row_count, copies, GROUPS, HEAD_DIM)
    normal_out = grouped * lax.rsqrt(mean_square + epsilon)
    mixed_out = (normal_out.reshape(row_count, inner_width) * norm_gain).astype(jnp.bfloat16)
    summed = lax.psum_scatter(
        jnp.dot(mixed_out, proj_output, preferred_element_type=jnp.float32).astype(jnp.bfloat16),
        "tp",
        scatter_dimension=0,
        tiled=True,
    ).astype(jnp.float32)
    return (tokens_wide + summed).astype(jnp.bfloat16)


def plain_solution(mesh):
    placed = (
        P(("dp", "seq", "tp"), None),
        P(),
        P(None, "tp"),
        P(None, "tp"),
        P(None, "tp"),
        P(None, "tp"),
        P("tp"),
        P("tp"),
        P(None, "tp"),
        P(None, "tp"),
        P("tp"),
        P("tp"),
        P("tp", None),
    )
    return jax.shard_map(
        plain_body, mesh=mesh, in_specs=placed, out_specs=P(("dp", "seq", "tp"), None), check_vma=False
    )


LANES = 128
PAD = 16
MESH = pl.DeviceIdType.MESH
NT = (((1,), (1,)), ((), ()))


def remote(source, target, send, receive, device):
    return pltpu.make_async_remote_copy(
        src_ref=source,
        dst_ref=target,
        send_sem=send,
        recv_sem=receive,
        device_id=device,
        device_id_type=MESH,
    )


def bdot(a, b):
    return jnp.dot(a, b, preferred_element_type=jnp.float32)


def fused_kernel(
    n,
    shards,
    tokens,
    pre_gain,
    w_inner,
    w_gate,
    w_states,
    w_step,
    step_bias,
    log_rate,
    taps_inner,
    taps_states,
    skip_gain,
    norm_gain,
    w_out,
    out,
    wide,
    step_w,
    wout,
    rows_all,
    proj,
    states,
    taps_all,
    raw_step,
    run_ref,
    x_mix,
    s_mix,
    acc,
    ends,
    state_out,
    state_in,
    squares,
    mixed,
    stage,
    from_right,
    from_left,
    load_sem,
    g_send,
    g_recv,
    t_send,
    t_recv,
    s_send,
    s_recv,
    ti_send,
    ti_recv,
    ts_send,
    ts_recv,
    e_send,
    e_recv,
    q_send,
    q_recv,
    r_send,
    rl_recv,
    rr_recv,
):
    z = lax.axis_index("tp")
    s = lax.axis_index("seq")
    rows, width = tokens.shape
    total = n * rows
    inner = w_inner.shape[1]
    state_w = w_states.shape[1]
    heads = w_step.shape[0]
    half = rows // 2

    barrier = pltpu.get_barrier_semaphore()

    def greet(i, _):
        other_s, other_z = i // n, lax.rem(i, n)

        @pl.when(jnp.logical_or(other_s != s, other_z != z))
        def _():
            pl.semaphore_signal(
                barrier, inc=1, device_id={"seq": other_s, "tp": other_z}, device_id_type=MESH
            )

        return 0

    lax.fori_loop(0, shards * n, greet, 0)
    loads = [
        pltpu.make_async_copy(w_states, wide.at[:, pl.ds(2 * inner, state_w)], load_sem.at[0]),
        pltpu.make_async_copy(w_step, step_w, load_sem.at[1]),
        pltpu.make_async_copy(w_inner, wide.at[:, pl.ds(0, inner)], load_sem.at[2]),
        pltpu.make_async_copy(w_gate, wide.at[:, pl.ds(inner, inner)], load_sem.at[3]),
        pltpu.make_async_copy(w_out, wout, load_sem.at[4]),
    ]
    for load in loads[:4]:
        load.start()

    def own_rows(i, _):
        piece = pl.ds(pl.multiple_of(i * 16, 16), 16)
        value = tokens[piece, :].astype(jnp.float32)
        scale = lax.rsqrt(jnp.mean(value * value, axis=1, keepdims=True) + epsilon)
        place = pl.ds(pl.multiple_of(z * rows + i * 16, 16), 16)
        rows_all[place, :] = (value * scale * pre_gain[...]).astype(jnp.bfloat16)
        return 0

    lax.fori_loop(0, rows // 16, own_rows, 0)
    taps_all[z] = taps_states[...]

    @pl.when(s == 0)
    def _():
        proj[0:PAD, 0:inner] = jnp.zeros((PAD, inner), jnp.bfloat16)
        states[0:PAD, :] = jnp.zeros((PAD, states.shape[1]), jnp.bfloat16)
        state_in[...] = jnp.zeros(state_in.shape, jnp.bfloat16)

    pl.semaphore_wait(barrier, shards * n - 1)

    def row_copy(source, part, side):
        block = rows_all.at[pl.ds(pl.multiple_of(source * rows + part * half, 16), half), :]
        step = 1 if side == 0 else -1
        return remote(
            block, block, g_send.at[side, source, part], g_recv.at[source, part], {"tp": z + step}
        )

    def send_on(source, part):
        @pl.when(jnp.logical_and(source <= z, z < n - 1))
        def _():
            row_copy(source, part, 0).start()

        @pl.when(jnp.logical_and(source >= z, z > 0))
        def _():
            row_copy(source, part, 1).start()

    for part in range(2):
        send_on(z, part)

    def tap_copy(source, other):
        return remote(
            taps_all.at[source], taps_all.at[source], t_send.at[other], t_recv.at[source], {"tp": other}
        )

    def state_copy(source, chunk, other):
        block = states.at[
            pl.ds(pl.multiple_of(PAD + chunk * rows, 16), rows),
            pl.ds(pl.multiple_of(source * state_w, LANES), state_w),
        ]
        return remote(
            block, block, s_send.at[chunk, other], s_recv.at[source, chunk], {"tp": other}
        )

    def square_copy(source, other):
        return remote(
            squares.at[source], squares.at[source], q_send.at[other], q_recv.at[source], {"tp": other}
        )

    def each_other(action):
        def one(i, _):
            @pl.when(i != z)
            def _():
                action(i)

            return 0

        lax.fori_loop(0, n, one, 0)

    each_other(lambda i: tap_copy(z, i).start())

    def inner_tail():
        return remote(
            proj.at[pl.ds(total, PAD), pl.ds(0, inner)],
            proj.at[pl.ds(0, PAD), pl.ds(0, inner)],
            ti_send,
            ti_recv,
            {"seq": s + 1, "tp": z},
        )

    def state_tail(source, other):
        columns = pl.ds(pl.multiple_of(source * state_w, LANES), state_w)
        return remote(
            states.at[pl.ds(total, PAD), columns],
            states.at[pl.ds(0, PAD), columns],
            ts_send.at[other],
            ts_recv.at[source],
            {"seq": s + 1, "tp": other},
        )

    for load in loads[:4]:
        load.wait()
    loads[4].start()

    def project_tiles(chunk, first, end):
        piece = pl.ds(pl.multiple_of(chunk * rows, rows), rows)
        place = pl.ds(pl.multiple_of(PAD + chunk * rows, 16), rows)

        def tile(i, _):
            columns = pl.ds(pl.multiple_of(i * 256, 256), 256)
            proj[place, columns] = bdot(rows_all[piece, :], wide[:, columns]).astype(jnp.bfloat16)
            return 0

        lax.fori_loop(first, end, tile, 0)

    def project(chunk, tiles):
        piece = pl.ds(pl.multiple_of(chunk * rows, rows), rows)
        place = pl.ds(pl.multiple_of(PAD + chunk * rows, 16), rows)
        own = pl.ds(pl.multiple_of(z * state_w, LANES), state_w)
        states[place, own] = bdot(
            rows_all[piece, :], wide[:, 2 * inner : 2 * inner + state_w]
        ).astype(jnp.bfloat16)
        each_other(lambda i: state_copy(z, chunk, i).start())

        @pl.when(jnp.logical_and(chunk == n - 1, s < shards - 1))
        def _():
            for other in range(n):
                state_tail(z, other).start()

        raw_step[piece, :] = lax.dot_general(
            rows_all[piece, :], step_w[...], NT, preferred_element_type=jnp.float32
        )

        project_tiles(chunk, 0, tiles)

        @pl.when(jnp.logical_and(chunk == n - 1, s < shards - 1))
        def _():
            inner_tail().start()

    gate_tile = inner // 256
    farthest = jnp.maximum(z, n - 1 - z)

    def arrive(distance, _):
        for side in range(2):
            source = z - distance if side == 0 else z + distance
            inside = jnp.logical_and(source >= 0, source < n)

            @pl.when(jnp.logical_and(inside, distance > 0))
            def _():
                for part in range(2):
                    row_copy(source, part, side).wait_recv()
                    send_on(source, part)

        def one(side, _):
            source = z - distance + 2 * distance * side
            inside = jnp.logical_and(source >= 0, source < n)

            @pl.when(jnp.logical_and(inside, jnp.logical_or(distance > 0, side == 0)))
            def _():
                project(source, jnp.where(distance == farthest, gate_tile, 2 * gate_tile))

            return 0

        lax.fori_loop(0, 2, one, 0)
        return 0

    lax.fori_loop(0, n, arrive, 0)

    def late_gate(side, _):
        source = z - farthest + 2 * farthest * side

        @pl.when(jnp.logical_and(source >= 0, source < n))
        def _():
            project_tiles(source, gate_tile, 2 * gate_tile)

        return 0

    lax.fori_loop(0, 2, late_gate, 0)

    step = raw_step[...] + step_bias[...]
    step = jnp.maximum(step, 0.0) + jnp.log1p(jnp.exp(-jnp.abs(step)))
    decay = -jnp.exp(log_rate[...]) * step
    place_t = lax.broadcasted_iota(jnp.int32, (total, total), 0)
    place_s = lax.broadcasted_iota(jnp.int32, (total, total), 1)
    tri = (place_t >= place_s).astype(jnp.float32)
    run = jnp.dot(tri, decay, precision=highest, preferred_element_type=jnp.float32)
    run_ref[...] = jnp.zeros(run_ref.shape, jnp.float32)
    run_ref[:, 0:heads] = run
    run_t = run_ref[...].T
    last = run[total - 1 : total, :]
    reach = jnp.exp(last - run) * step
    grown = jnp.exp(run)
    whole = jnp.exp(last)
    lane = lax.broadcasted_iota(jnp.int32, (1, LANES), 1)
    low = lane < HEAD_DIM

    def conv(buffer, columns, taps):
        value = buffer[:, columns].astype(jnp.float32)
        kernel_len = taps.shape[0]
        out_value = jnp.zeros((total, value.shape[1]), jnp.float32)
        for k in range(kernel_len):
            first = PAD - (kernel_len - 1) + k
            out_value = out_value + taps[k : k + 1, :] * value[first : first + total, :]
        return jax.nn.silu(out_value).astype(jnp.bfloat16)

    @pl.when(s > 0)
    def _():
        inner_tail().wait_recv()

    def conv_tile(i, _):
        columns = pl.ds(pl.multiple_of(i * 256, 256), 256)
        x_mix[:, columns] = conv(proj, columns, taps_inner[:, columns])
        return 0

    lax.fori_loop(0, inner // 256, conv_tile, 0)

    def take_states(i, _):
        @pl.when(i != z)
        def _():
            tap_copy(i, z).wait_recv()
            for chunk in range(n):
                state_copy(i, chunk, z).wait_recv()

        @pl.when(s > 0)
        def _():
            state_tail(i, z).wait_recv()

        columns = pl.ds(pl.multiple_of(i * state_w, LANES), state_w)
        s_mix[:, columns] = conv(states, columns, taps_all[i])
        return 0

    lax.fori_loop(0, n, take_states, 0)

    def group_in(g):
        return s_mix[:, g * 2 * STATE : g * 2 * STATE + STATE]

    def group_out(g):
        return s_mix[:, g * 2 * STATE + STATE : (g + 1) * 2 * STATE]

    def pair_of(value, h):
        return jnp.where(low, value[:, h : h + 1], value[:, h + 1 : h + 2])

    pairs = heads // 2
    per_quad = GROUPS // 2
    quads = pairs // per_quad
    quad_w = GROUPS * HEAD_DIM

    turned = [group_in(g).T for g in range(GROUPS)]
    for q in range(pairs):
        columns = slice(q * LANES, (q + 1) * LANES)
        h = 2 * q
        scaled = (x_mix[:, columns].astype(jnp.float32) * pair_of(reach, h)).astype(jnp.bfloat16)
        ends[:, columns] = jnp.where(
            low, bdot(turned[h % GROUPS], scaled), bdot(turned[(h + 1) % GROUPS], scaled)
        )

    def end_copy(c):
        columns = pl.ds(c * quad_w, quad_w)
        return remote(
            state_out.at[:, columns],
            state_in.at[:, columns],
            e_send.at[c],
            e_recv.at[c],
            {"seq": s + 1, "tp": z},
        )

    @pl.when(jnp.logical_and(s == 0, shards > 1))
    def _():
        for c in range(quads):
            columns = slice(c * quad_w, (c + 1) * quad_w)
            state_out[:, columns] = ends[:, columns].astype(jnp.bfloat16)
            end_copy(c).start()

    def hand_on(c):
        @pl.when(s > 0)
        def _():
            end_copy(c).wait_recv()

            @pl.when(s < shards - 1)
            def _():
                for q in range(c * per_quad, (c + 1) * per_quad):
                    columns = slice(q * LANES, (q + 1) * LANES)
                    state_out[:, columns] = (
                        ends[:, columns]
                        + pair_of(whole, 2 * q) * state_in[:, columns].astype(jnp.float32)
                    ).astype(jnp.bfloat16)
                end_copy(c).start()

    scores = [
        lax.dot_general(group_out(g), group_in(g), NT, preferred_element_type=jnp.float32)
        for g in range(GROUPS)
    ]
    for q in range(pairs):
        columns = slice(q * LANES, (q + 1) * LANES)
        h = 2 * q
        value = x_mix[:, columns].astype(jnp.float32)
        stepped = (value * pair_of(step, h)).astype(jnp.bfloat16)
        direct = value * pair_of(skip_gain[...], h)
        for low_t in range(0, total, BLOCK):
            high_t = low_t + BLOCK
            causal = place_t[low_t:high_t, :high_t] >= place_s[low_t:high_t, :high_t]
            both = []
            for k in (h, h + 1):
                spread = run[low_t:high_t, k : k + 1] - run_t[k : k + 1, :high_t]
                table = jnp.where(causal, jnp.exp(jnp.where(causal, spread, 0.0)), 0.0)
                weights = (scores[k % GROUPS][low_t:high_t, :high_t] * table).astype(jnp.bfloat16)
                both.append(bdot(weights, stepped[:high_t, :]))
            acc[low_t:high_t, columns] = jnp.where(low, both[0], both[1]) + direct[low_t:high_t, :]
        if q % per_quad == per_quad - 1:
            hand_on(q // per_quad)

    sums = [jnp.zeros((total, LANES), jnp.float32) for _ in range(per_quad)]
    for q in range(pairs):
        columns = slice(q * LANES, (q + 1) * LANES)
        h = 2 * q
        came = state_in[:, columns]
        carried = jnp.where(
            low, bdot(group_out(h % GROUPS), came), bdot(group_out((h + 1) % GROUPS), came)
        )
        gate = proj[PAD:, inner + q * LANES : inner + (q + 1) * LANES].astype(jnp.float32)
        gated = (acc[:, columns] + carried * pair_of(grown, h)) * jax.nn.silu(gate)
        acc[:, columns] = gated
        sums[q % per_quad] = sums[q % per_quad] + gated * gated
    pick = lax.broadcasted_iota(jnp.int32, (8, LANES), 0)
    where_lane = lax.broadcasted_iota(jnp.int32, (8, LANES), 1)
    local = jnp.zeros((8, total), jnp.float32)
    for k in range(per_quad):
        chosen = (where_lane // HEAD_DIM + 2 * k == pick).astype(jnp.float32)
        local = local + lax.dot_general(
            chosen, sums[k], NT, precision=highest, preferred_element_type=jnp.float32
        )
    squares[z] = local
    each_other(lambda i: square_copy(z, i).start())
    loads[4].wait()
    each_other(lambda i: square_copy(i, z).wait_recv())
    sum_all = squares[0]
    for i in range(1, n):
        sum_all = sum_all + squares[i]
    inverse = lax.rsqrt(sum_all / (n * heads // GROUPS * HEAD_DIM) + epsilon)
    inverse = jnp.concatenate([inverse] * (LANES // 8), axis=0).T
    for q in range(pairs):
        columns = slice(q * LANES, (q + 1) * LANES)
        g = (2 * q) % GROUPS
        mixed[:, columns] = (
            acc[:, columns] * pair_of(inverse, g) * norm_gain[:, columns]
        ).astype(jnp.bfloat16)

    pieces = r_send.shape[1]
    piece_w = width // pieces

    def partial_of(target, p):
        return bdot(mixed[pl.ds(pl.multiple_of(target * rows, rows), rows), :], wout[:, p])

    def columns_of(p):
        return pl.ds(pl.multiple_of(p * piece_w, LANES), piece_w)

    def sum_copy(target, p, side):
        landing, receive, way = (from_right, rl_recv, -1) if side == 0 else (from_left, rr_recv, 1)
        return remote(
            stage.at[target, :, columns_of(p)],
            landing.at[target, :, columns_of(p)],
            r_send.at[target, p],
            receive.at[target, p],
            {"tp": z + way},
        )

    items = (n - 1) * pieces
    lag = 3

    def one_sum(t, _):
        for side in range(2):
            i = t - lag * (n - 1 - z) if side == 0 else t - lag * z
            k, p = jnp.maximum(i, 0) // pieces, lax.rem(jnp.maximum(i, 0), pieces)
            target = k if side == 0 else n - 1 - k
            landing = from_right if side == 0 else from_left
            active = target < z if side == 0 else target > z
            more = z < n - 1 if side == 0 else z > 0
            active = jnp.logical_and(active, jnp.logical_and(i >= 0, i < items))

            @pl.when(active)
            def _():
                value = partial_of(target, columns_of(p))

                @pl.when(more)
                def _():
                    sum_copy(target, p, side).wait_recv()
                    stage[target, :, columns_of(p)] = (
                        value + landing[target, :, columns_of(p)].astype(jnp.float32)
                    ).astype(jnp.bfloat16)

                @pl.when(jnp.logical_not(more))
                def _():
                    stage[target, :, columns_of(p)] = value.astype(jnp.bfloat16)

                sum_copy(target, p, side).start()

        return 0

    lax.fori_loop(0, items + lag * (n - 1), one_sum, 0)

    def finish(p, _):
        columns = columns_of(p)
        acc_out = tokens[:, columns].astype(jnp.float32) + partial_of(z, columns)
        stage[z, :, columns] = acc_out.astype(jnp.bfloat16)

        @pl.when(z < n - 1)
        def _():
            sum_copy(z, p, 0).wait_recv()

        @pl.when(z > 0)
        def _():
            sum_copy(z, p, 1).wait_recv()

        none = jnp.zeros((rows, piece_w), jnp.float32)
        right = jnp.where(z < n - 1, from_right[z, :, columns].astype(jnp.float32), none)
        left = jnp.where(z > 0, from_left[z, :, columns].astype(jnp.float32), none)
        out[:, columns] = (acc_out + right + left).astype(jnp.bfloat16)
        return 0

    lax.fori_loop(0, pieces, finish, 0)

    def sent_rows(source, _):
        for part in range(2):

            @pl.when(jnp.logical_and(source <= z, z < n - 1))
            def _():
                row_copy(source, part, 0).wait_send()

            @pl.when(jnp.logical_and(source >= z, z > 0))
            def _():
                row_copy(source, part, 1).wait_send()

        return 0

    lax.fori_loop(0, n, sent_rows, 0)

    def sent_small(i):
        tap_copy(z, i).wait_send()
        square_copy(z, i).wait_send()
        for chunk in range(n):
            state_copy(z, chunk, i).wait_send()

        def sent_sum(p, _):
            sum_copy(i, p, 0).wait_send()
            return 0

        lax.fori_loop(0, pieces, sent_sum, 0)

    each_other(sent_small)

    @pl.when(s < shards - 1)
    def _():
        inner_tail().wait_send()
        for other in range(n):
            state_tail(z, other).wait_send()
        for c in range(quads):
            end_copy(c).wait_send()


def body(
    n,
    shards,
    tokens,
    pre_gain,
    proj_inner,
    proj_gate,
    proj_states,
    proj_step,
    step_bias,
    log_rate,
    conv_inner,
    conv_states,
    skip_gain,
    norm_gain,
    proj_output,
):
    rows, width = tokens.shape
    inner, state_w, heads = proj_inner.shape[1], proj_states.shape[1], proj_step.shape[1]
    total = n * rows
    all_states = n * state_w
    quads = heads // GROUPS
    pieces = 8
    bf16, f32 = jnp.bfloat16, jnp.float32
    vmem = pl.BlockSpec(memory_space=pltpu.VMEM)
    far = pl.BlockSpec(memory_space=pl.ANY)
    dma = pltpu.SemaphoreType.DMA
    return pl.pallas_call(
        partial(fused_kernel, n, shards),
        out_shape=jax.ShapeDtypeStruct((rows, width), bf16),
        in_specs=[vmem, vmem, far, far, far, far, vmem, vmem, vmem, vmem, vmem, vmem, far],
        out_specs=vmem,
        scratch_shapes=[
            pltpu.VMEM((width, 2 * inner + state_w), bf16),
            pltpu.VMEM((heads, width), bf16),
            pltpu.VMEM((inner, width), bf16),
            pltpu.VMEM((total, width), bf16),
            pltpu.VMEM((PAD + total, 2 * inner), bf16),
            pltpu.VMEM((PAD + total, all_states), bf16),
            pltpu.VMEM((n,) + conv_states.shape, f32),
            pltpu.VMEM((total, heads), f32),
            pltpu.VMEM((total, LANES), f32),
            pltpu.VMEM((total, inner), bf16),
            pltpu.VMEM((total, all_states), bf16),
            pltpu.VMEM((total, inner), f32),
            pltpu.VMEM((STATE, inner), f32),
            pltpu.VMEM((STATE, inner), bf16),
            pltpu.VMEM((STATE, inner), bf16),
            pltpu.VMEM((n, 8, total), f32),
            pltpu.VMEM((total, inner), bf16),
            pltpu.VMEM((n, rows, width), bf16),
            pltpu.VMEM((n, rows, width), bf16),
            pltpu.VMEM((n, rows, width), bf16),
            dma((5,)),
            dma((2, n, 2)),
            dma((n, 2)),
            dma((n,)),
            dma((n,)),
            dma((n, n)),
            dma((n, n)),
            dma,
            dma,
            dma((n,)),
            dma((n,)),
            dma((quads,)),
            dma((quads,)),
            dma((n,)),
            dma((n,)),
            dma((n, pieces)),
            dma((n, pieces)),
            dma((n, pieces)),
        ],
        compiler_params=pltpu.CompilerParams(
            collective_id=0, has_side_effects=True, vmem_limit_bytes=62 * 1024 * 1024
        ),
    )(
        tokens,
        pre_gain[None],
        proj_inner,
        proj_gate,
        proj_states,
        proj_step.T,
        step_bias[None],
        log_rate[None],
        conv_inner,
        conv_states,
        skip_gain[None],
        norm_gain[None],
        proj_output,
    )


def solution(mesh):
    n, shards = mesh.shape["tp"], mesh.shape["seq"]
    plain = plain_solution(mesh)

    def run(*arrays):
        tokens, proj_inner, proj_states, proj_step = arrays[0], arrays[2], arrays[4], arrays[5]
        rows = tokens.shape[0] // (mesh.shape["dp"] * shards * n)
        heads, state_w = proj_step.shape[1] // n, proj_states.shape[1] // n
        fits = (
            rows % 32 == 0
            and (rows * n) % BLOCK == 0
            and state_w % LANES == 0
            and heads % GROUPS == 0
            and (proj_inner.shape[1] // n) % 256 == 0
        )
        if not fits:
            return plain(*arrays)
        line = P(("dp", "seq", "tp"), None)
        columns = P(None, "tp")
        placed = (
            (line, P()) + (columns,) * 4 + (P("tp"), P("tp"), columns, columns)
            + (P("tp"), P("tp"), P("tp", None))
        )
        return jax.shard_map(
            partial(body, n, shards), mesh=mesh, in_specs=placed, out_specs=line, check_vma=False
        )(*arrays)

    return run
```

profile of v0, /device:TPU:10, one launch (start us, length us, event | category | flops | bytes accessed | tf_op | source)
XLA Modules:
  0.0 107.8 jit_solution(5066352596201356007)
XLA Ops:
  0.0 105.9 %shard_map.127 = bf16[64,4096]{1,0:T(8,128)(2,1)} custom-call(bf16[64,4096]{1,0:T(8,128)(2,1)} %tokens.1, f32[1,4096]{1,0:T(1,128)} %bitcast.7, bf16[4096,1024]{1,0:T(8,128)(2,1)} %w_inner.1, bf16[4096,1024]{1,0:T(8,128)(2,1)} %w_gate.1, bf16[4096,256]{1,0:T(8,128)(2,1)} %w_states.1, bf16[16,4096]{1,0:T(8,128)(2,1)} %bitcast.6, f32[1,16]{1,0:T(1,128)} %bitcast.9, ...), custom_call_target="tpu_custom_call" | custom-call | tf_op jit(solution)/shard_map/pallas_call | solution.py:796
  105.9 1.9 %copy.15 = bf16[64,4096]{1,0:T(8,128)(2,1)} copy(bf16[64,4096]{1,0:T(8,128)(2,1)} %shard_map.127) | data formatting | bytes 1048576
where the time goes:
time: 108 us
  Pallas kernels  106 us (98%)
  local copies, waits for them, and re-layouts  1.87 us (2%)
    pallas_call x1, Pallas kernels, body(): pl.pallas_call(partial(fused_kernel, n, shards), out_shape=jax.ShapeDtype...  106 us

commit v1 on v0

--- a/solution.py
+++ b/solution.py
@@ -233,7 +233,7 @@
 def fused_kernel(
     n,
     shards,
-    tokens,
+    tokens_far,
     pre_gain,
     w_inner,
     w_gate,
@@ -247,6 +247,7 @@
     norm_gain,
     w_out,
     out,
+    tokens,
     wide,
     step_w,
     wout,
@@ -267,13 +268,18 @@
     stage,
     from_right,
     from_left,
+    own_sum,
     load_sem,
+    line,
+    ahead,
     g_send,
     g_recv,
     t_send,
     t_recv,
     s_send,
     s_recv,
+    c_send,
+    c_recv,
     ti_send,
     ti_recv,
     ts_send,
@@ -295,20 +301,23 @@
     heads = w_step.shape[0]
     half = rows // 2
 
+    token_load = pltpu.make_async_copy(tokens_far, tokens, load_sem.at[5])
+    token_load.start()
     barrier = pltpu.get_barrier_semaphore()
-
-    def greet(i, _):
-        other_s, other_z = i // n, lax.rem(i, n)
-
-        @pl.when(jnp.logical_or(other_s != s, other_z != z))
-        def _():
-            pl.semaphore_signal(
-                barrier, inc=1, device_id={"seq": other_s, "tp": other_z}, device_id_type=MESH
-            )
-
-        return 0
-
-    lax.fori_loop(0, shards * n, greet, 0)
+    neighbours = (
+        (z > 0, {"tp": z - 1}),
+        (z < n - 1, {"tp": z + 1}),
+        (s > 0, {"seq": s - 1}),
+        (s < shards - 1, {"seq": s + 1}),
+    )
+    met = jnp.int32(0)
+    for there, device in neighbours:
+        met = met + there.astype(jnp.int32)
+
+        @pl.when(there)
+        def _():
+            pl.semaphore_signal(barrier, inc=1, device_id=device, device_id_type=MESH)
+
     loads = [
         pltpu.make_async_copy(w_states, wide.at[:, pl.ds(2 * inner, state_w)], load_sem.at[0]),
         pltpu.make_async_copy(w_step, step_w, load_sem.at[1]),
@@ -316,6 +325,7 @@
         pltpu.make_async_copy(w_gate, wide.at[:, pl.ds(inner, inner)], load_sem.at[3]),
         pltpu.make_async_copy(w_out, wout, load_sem.at[4]),
     ]
+    token_load.wait()
     for load in loads[:4]:
         load.start()
 
@@ -327,7 +337,7 @@
         rows_all[place, :] = (value * scale * pre_gain[...]).astype(jnp.bfloat16)
         return 0
 
-    lax.fori_loop(0, rows // 16, own_rows, 0)
+    lax.fori_loop(0, half // 16, own_rows, 0)
     taps_all[z] = taps_states[...]
 
     @pl.when(s == 0)
@@ -336,7 +346,7 @@
         states[0:PAD, :] = jnp.zeros((PAD, states.shape[1]), jnp.bfloat16)
         state_in[...] = jnp.zeros(state_in.shape, jnp.bfloat16)
 
-    pl.semaphore_wait(barrier, shards * n - 1)
+    pl.semaphore_wait(barrier, met)
 
     def row_copy(source, part, side):
         block = rows_all.at[pl.ds(pl.multiple_of(source * rows + part * half, 16), half), :]
@@ -354,22 +364,55 @@
         def _():
             row_copy(source, part, 1).start()
 
-    for part in range(2):
-        send_on(z, part)
+    send_on(z, 0)
+    lax.fori_loop(half // 16, rows // 16, own_rows, 0)
+    send_on(z, 1)
+
+    def greet_line(side, condition):
+        @pl.when(condition)
+        def _():
+            pl.semaphore_signal(
+                line.at[side],
+                inc=1,
+                device_id={"tp": z + 1 if side == 0 else z - 1},
+                device_id_type=MESH,
+            )
+
+    greet_line(0, z == 0)
+    greet_line(1, z == n - 1)
+    for side in range(2):
+        edge = 0 if side == 0 else n - 1
+
+        @pl.when(z != edge)
+        def _():
+            pl.semaphore_wait(line.at[side], 1)
+
+        greet_line(side, jnp.logical_and(z != edge, z != n - 1 - edge))
+
+    @pl.when(s > 0)
+    def _():
+        pl.semaphore_signal(ahead, inc=1, device_id={"seq": s - 1}, device_id_type=MESH)
+
 
     def tap_copy(source, other):
         return remote(
             taps_all.at[source], taps_all.at[source], t_send.at[other], t_recv.at[source], {"tp": other}
         )
 
-    def state_copy(source, chunk, other):
+    def in_copy(source, chunk, other):
         block = states.at[
             pl.ds(pl.multiple_of(PAD + chunk * rows, 16), rows),
-            pl.ds(pl.multiple_of(source * state_w, LANES), state_w),
+            pl.ds(pl.multiple_of(source * state_w, LANES), STATE),
         ]
         return remote(
             block, block, s_send.at[chunk, other], s_recv.at[source, chunk], {"tp": other}
         )
+
+    def out_copy(source, other):
+        block = states.at[
+            pl.ds(PAD, total), pl.ds(pl.multiple_of(source * state_w + STATE, LANES), STATE)
+        ]
+        return remote(block, block, c_send.at[other], c_recv.at[source], {"tp": other})
 
     def square_copy(source, other):
         return remote(
@@ -429,10 +472,11 @@
         states[place, own] = bdot(
             rows_all[piece, :], wide[:, 2 * inner : 2 * inner + state_w]
         ).astype(jnp.bfloat16)
-        each_other(lambda i: state_copy(z, chunk, i).start())
+        each_other(lambda i: in_copy(z, chunk, i).start())
 
         @pl.when(jnp.logical_and(chunk == n - 1, s < shards - 1))
         def _():
+            pl.semaphore_wait(ahead, 1)
             for other in range(n):
                 state_tail(z, other).start()
 
@@ -484,7 +528,7 @@
 
         return 0
 
-    lax.fori_loop(0, 2, late_gate, 0)
+    each_other(lambda i: out_copy(z, i).start())
 
     step = raw_step[...] + step_bias[...]
     step = jnp.maximum(step, 0.0) + jnp.log1p(jnp.exp(-jnp.abs(step)))
@@ -523,22 +567,34 @@
 
     lax.fori_loop(0, inner // 256, conv_tile, 0)
 
-    def take_states(i, _):
+    def take_states(part, i):
+        columns = pl.ds(pl.multiple_of(i * state_w + part * STATE, LANES), STATE)
+        taps = taps_all[i][:, part * STATE : (part + 1) * STATE]
+        s_mix[:, columns] = conv(states, columns, taps)
+
+    def take_in(i, _):
         @pl.when(i != z)
         def _():
             tap_copy(i, z).wait_recv()
             for chunk in range(n):
-                state_copy(i, chunk, z).wait_recv()
+                in_copy(i, chunk, z).wait_recv()
 
         @pl.when(s > 0)
         def _():
             state_tail(i, z).wait_recv()
 
-        columns = pl.ds(pl.multiple_of(i * state_w, LANES), state_w)
-        s_mix[:, columns] = conv(states, columns, taps_all[i])
+        take_states(0, i)
         return 0
 
-    lax.fori_loop(0, n, take_states, 0)
+    def take_out(i, _):
+        @pl.when(i != z)
+        def _():
+            out_copy(i, z).wait_recv()
+
+        take_states(1, i)
+        return 0
+
+    lax.fori_loop(0, n, take_in, 0)
 
     def group_in(g):
         return s_mix[:, g * 2 * STATE : g * 2 * STATE + STATE]
@@ -553,15 +609,6 @@
     per_quad = GROUPS // 2
     quads = pairs // per_quad
     quad_w = GROUPS * HEAD_DIM
-
-    turned = [group_in(g).T for g in range(GROUPS)]
-    for q in range(pairs):
-        columns = slice(q * LANES, (q + 1) * LANES)
-        h = 2 * q
-        scaled = (x_mix[:, columns].astype(jnp.float32) * pair_of(reach, h)).astype(jnp.bfloat16)
-        ends[:, columns] = jnp.where(
-            low, bdot(turned[h % GROUPS], scaled), bdot(turned[(h + 1) % GROUPS], scaled)
-        )
 
     def end_copy(c):
         columns = pl.ds(c * quad_w, quad_w)
@@ -573,15 +620,25 @@
             {"seq": s + 1, "tp": z},
         )
 
-    @pl.when(jnp.logical_and(s == 0, shards > 1))
-    def _():
-        for c in range(quads):
-            columns = slice(c * quad_w, (c + 1) * quad_w)
-            state_out[:, columns] = ends[:, columns].astype(jnp.bfloat16)
-            end_copy(c).start()
-
-    def hand_on(c):
-        @pl.when(s > 0)
+    turned = [group_in(g).T for g in range(GROUPS)]
+    for q in range(pairs):
+        columns = slice(q * LANES, (q + 1) * LANES)
+        h = 2 * q
+        scaled = (x_mix[:, columns].astype(jnp.float32) * pair_of(reach, h)).astype(jnp.bfloat16)
+        ends[:, columns] = jnp.where(
+            low, bdot(turned[h % GROUPS], scaled), bdot(turned[(h + 1) % GROUPS], scaled)
+        )
+        if q % per_quad == per_quad - 1:
+            c = q // per_quad
+
+            @pl.when(jnp.logical_and(s == 0, shards > 1))
+            def _():
+                columns = slice(c * quad_w, (c + 1) * quad_w)
+                state_out[:, columns] = ends[:, columns].astype(jnp.bfloat16)
+                end_copy(c).start()
+
+    def hand_on(c, here):
+        @pl.when(here)
         def _():
             end_copy(c).wait_recv()
 
@@ -594,6 +651,11 @@
                         + pair_of(whole, 2 * q) * state_in[:, columns].astype(jnp.float32)
                     ).astype(jnp.bfloat16)
                 end_copy(c).start()
+
+    lax.fori_loop(0, 2, late_gate, 0)
+    for c in range(quads):
+        hand_on(c, s == 1)
+    lax.fori_loop(0, n, take_out, 0)
 
     scores = [
         lax.dot_general(group_out(g), group_in(g), NT, preferred_element_type=jnp.float32)
@@ -615,13 +677,12 @@
                 weights = (scores[k % GROUPS][low_t:high_t, :high_t] * table).astype(jnp.bfloat16)
                 both.append(bdot(weights, stepped[:high_t, :]))
             acc[low_t:high_t, columns] = jnp.where(low, both[0], both[1]) + direct[low_t:high_t, :]
-        if q % per_quad == per_quad - 1:
-            hand_on(q // per_quad)
-
     sums = [jnp.zeros((total, LANES), jnp.float32) for _ in range(per_quad)]
     for q in range(pairs):
         columns = slice(q * LANES, (q + 1) * LANES)
         h = 2 * q
+        if q % per_quad == 0:
+            hand_on(q // per_quad, s > 1)
         came = state_in[:, columns]
         carried = jnp.where(
             low, bdot(group_out(h % GROUPS), came), bdot(group_out((h + 1) % GROUPS), came)
@@ -703,15 +764,17 @@
 
                 sum_copy(target, p, side).start()
 
+        @pl.when(jnp.logical_and(t >= items, t < items + pieces))
+        def _():
+            columns = columns_of(t - items)
+            own_sum[:, columns] = tokens[:, columns].astype(jnp.float32) + partial_of(z, columns)
+
         return 0
 
-    lax.fori_loop(0, items + lag * (n - 1), one_sum, 0)
+    lax.fori_loop(0, items + max(lag * (n - 1), pieces), one_sum, 0)
 
     def finish(p, _):
         columns = columns_of(p)
-        acc_out = tokens[:, columns].astype(jnp.float32) + partial_of(z, columns)
-        stage[z, :, columns] = acc_out.astype(jnp.bfloat16)
-
         @pl.when(z < n - 1)
         def _():
             sum_copy(z, p, 0).wait_recv()
@@ -723,7 +786,7 @@
         none = jnp.zeros((rows, piece_w), jnp.float32)
         right = jnp.where(z < n - 1, from_right[z, :, columns].astype(jnp.float32), none)
         left = jnp.where(z > 0, from_left[z, :, columns].astype(jnp.float32), none)
-        out[:, columns] = (acc_out + right + left).astype(jnp.bfloat16)
+        out[:, columns] = (own_sum[:, columns] + right + left).astype(jnp.bfloat16)
         return 0
 
     lax.fori_loop(0, pieces, finish, 0)
@@ -746,8 +809,9 @@
     def sent_small(i):
         tap_copy(z, i).wait_send()
         square_copy(z, i).wait_send()
+        out_copy(z, i).wait_send()
         for chunk in range(n):
-            state_copy(z, chunk, i).wait_send()
+            in_copy(z, chunk, i).wait_send()
 
         def sent_sum(p, _):
             sum_copy(i, p, 0).wait_send()
@@ -796,9 +860,10 @@
     return pl.pallas_call(
         partial(fused_kernel, n, shards),
         out_shape=jax.ShapeDtypeStruct((rows, width), bf16),
-        in_specs=[vmem, vmem, far, far, far, far, vmem, vmem, vmem, vmem, vmem, vmem, far],
+        in_specs=[far, vmem, far, far, far, far, vmem, vmem, vmem, vmem, vmem, vmem, far],
         out_specs=vmem,
         scratch_shapes=[
+            pltpu.VMEM((rows, width), bf16),
             pltpu.VMEM((width, 2 * inner + state_w), bf16),
             pltpu.VMEM((heads, width), bf16),
             pltpu.VMEM((inner, width), bf16),
@@ -819,13 +884,18 @@
             pltpu.VMEM((n, rows, width), bf16),
             pltpu.VMEM((n, rows, width), bf16),
             pltpu.VMEM((n, rows, width), bf16),
-            dma((5,)),
+            pltpu.VMEM((rows, width), f32),
+            dma((6,)),
+            pltpu.SemaphoreType.REGULAR((2,)),
+            pltpu.SemaphoreType.REGULAR,
             dma((2, n, 2)),
             dma((n, 2)),
             dma((n,)),
             dma((n,)),
             dma((n, n)),
             dma((n, n)),
+            dma((n,)),
+            dma((n,)),
             dma,
             dma,
             dma((n,)),
@@ -869,7 +939,7 @@
         fits = (
             rows % 32 == 0
             and (rows * n) % BLOCK == 0
-            and state_w % LANES == 0
+            and state_w == 2 * STATE
             and heads % GROUPS == 0
             and (proj_inner.shape[1] // n) % 256 == 0
         )

time: 108 us -> 105 us (0.972)
  Pallas kernels: 106 us -> 103 us
    pallas_call x1, Pallas kernels: 106 us -> 103 us  [body(): pl.pallas_call(partial(fused_kernel, n, shards), out_shape=jax.ShapeDtype...]
where the time goes in v1:
time: 105 us; the launch traced here: 104 us
  Pallas kernels  103 us (98%)
  local copies, waits for them, and re-layouts  1.87 us (2%)
    pallas_call x1, Pallas kernels, body(): pl.pallas_call(partial(fused_kernel, n, shards), out_shape=jax.ShapeDtype...  103 us

profile of v1, /device:TPU:10, one launch (start us, length us, event | category | flops | bytes accessed | tf_op | source)
XLA Modules:
  0.0 104.5 jit_solution(11664737363505619842)
XLA Ops:
  0.0 102.6 %shard_map.127 = bf16[64,4096]{1,0:T(8,128)(2,1)} custom-call(bf16[64,4096]{1,0:T(8,128)(2,1)} %tokens_far.1, f32[1,4096]{1,0:T(1,128)} %bitcast.7, bf16[4096,1024]{1,0:T(8,128)(2,1)} %w_inner.1, bf16[4096,1024]{1,0:T(8,128)(2,1)} %w_gate.1, bf16[4096,256]{1,0:T(8,128)(2,1)} %w_states.1, bf16[16,4096]{1,0:T(8,128)(2,1)} %bitcast.6, f32[1,16]{1,0:T(1,128)} %bitcast.9, ...), custom_call_target="tpu_custom_call" | custom-call | tf_op jit(solution)/shard_map/pallas_call | solution.py:860
  102.6 1.9 %copy.15 = bf16[64,4096]{1,0:T(8,128)(2,1)} copy(bf16[64,4096]{1,0:T(8,128)(2,1)} %shard_map.127) | data formatting | bytes 1048576

commit v2 on v1

--- a/solution.py
+++ b/solution.py
@@ -233,6 +233,7 @@
 def fused_kernel(
     n,
     shards,
+    shared,
     tokens_far,
     pre_gain,
     w_inner,
@@ -269,6 +270,9 @@
     from_right,
     from_left,
     own_sum,
+    spare,
+    pre,
+    far,
     load_sem,
     line,
     ahead,
@@ -291,15 +295,30 @@
     r_send,
     rl_recv,
     rr_recv,
+    wz_send,
+    wz_recv,
+    wy_send,
+    wy_recv,
+    wx_send,
+    wx_recv,
+    wd_send,
+    wd_recv,
+    m_send,
+    m_recv,
 ):
     z = lax.axis_index("tp")
     s = lax.axis_index("seq")
+    part_id = lax.axis_index("dp")
     rows, width = tokens.shape
     total = n * rows
     inner = w_inner.shape[1]
     state_w = w_states.shape[1]
     heads = w_step.shape[0]
     half = rows // 2
+    at_end = jnp.logical_or(z == 0, z == n - 1)
+    beside = jnp.logical_or(z == 1, z == n - 2)
+    across = lax.rem(s + shards // 2, shards)
+    sibling = s + 1 - 2 * lax.rem(s, 2)
 
     token_load = pltpu.make_async_copy(tokens_far, tokens, load_sem.at[5])
     token_load.start()
@@ -309,6 +328,8 @@
         (z < n - 1, {"tp": z + 1}),
         (s > 0, {"seq": s - 1}),
         (s < shards - 1, {"seq": s + 1}),
+        (z >= 0, {"seq": across}),
+        (z >= 0, {"dp": 1 - part_id}),
     )
     met = jnp.int32(0)
     for there, device in neighbours:
@@ -364,9 +385,55 @@
         def _():
             row_copy(source, part, 1).start()
 
+    slice_rows = inner // (2 * shards)
+    chunk_rows = slice_rows // 2
+    shared_w = spare.shape[1]
+
+    def slice_of(d, q, c):
+        first = (d * shards + q) * slice_rows + c * chunk_rows
+        return pl.ds(pl.multiple_of(first, chunk_rows), chunk_rows)
+
+    def down_copy(c):
+        block = slice_of(part_id, s, c)
+        return remote(
+            w_out.at[block, pl.ds(0, shared_w)],
+            spare.at[block, :],
+            wz_send.at[c],
+            wz_recv.at[c],
+            {"tp": jnp.where(z == 0, 1, n - 2)},
+        )
+
+    def y_copy(c):
+        block = spare.at[slice_of(part_id, s, c), :]
+        return remote(block, block, wy_send.at[c], wy_recv.at[c], {"dp": 1 - part_id})
+
+    def y_taken(c):
+        block = spare.at[slice_of(1 - part_id, s, c), :]
+        return remote(block, block, wy_send.at[c], wy_recv.at[c], {"dp": 1 - part_id})
+
+    def x_copy(k, c, to):
+        d = part_id if k == 0 else 1 - part_id
+        block = spare.at[slice_of(d, s if to else across, c), :]
+        return remote(block, block, wx_send.at[k, c], wx_recv.at[k, c], {"seq": across})
+
+    def core_copy(j, to):
+        d = part_id if j % 2 == 0 else 1 - part_id
+        q = s if j < 2 else across
+        q = q if to else q + 1 - 2 * lax.rem(q, 2)
+        first = (d * shards + q) * slice_rows
+        block = spare.at[pl.ds(pl.multiple_of(first, slice_rows), slice_rows), :]
+        return remote(block, block, wd_send.at[j], wd_recv.at[j], {"seq": sibling})
+
+    def send_down(c):
+        @pl.when(at_end)
+        def _():
+            down_copy(c).start()
+
     send_on(z, 0)
+    send_down(0)
     lax.fori_loop(half // 16, rows // 16, own_rows, 0)
     send_on(z, 1)
+    send_down(1)
 
     def greet_line(side, condition):
         @pl.when(condition)
@@ -454,6 +521,8 @@
         load.wait()
     loads[4].start()
 
+    gate_tile = inner // 256
+
     def project_tiles(chunk, first, end):
         piece = pl.ds(pl.multiple_of(chunk * rows, rows), rows)
         place = pl.ds(pl.multiple_of(PAD + chunk * rows, 16), rows)
@@ -465,7 +534,7 @@
 
         lax.fori_loop(first, end, tile, 0)
 
-    def project(chunk, tiles):
+    def project(chunk):
         piece = pl.ds(pl.multiple_of(chunk * rows, rows), rows)
         place = pl.ds(pl.multiple_of(PAD + chunk * rows, 16), rows)
         own = pl.ds(pl.multiple_of(z * state_w, LANES), state_w)
@@ -484,25 +553,44 @@
             rows_all[piece, :], step_w[...], NT, preferred_element_type=jnp.float32
         )
 
-        project_tiles(chunk, 0, tiles)
+        project_tiles(chunk, 0, gate_tile)
 
         @pl.when(jnp.logical_and(chunk == n - 1, s < shards - 1))
         def _():
             inner_tail().start()
 
-    gate_tile = inner // 256
-    farthest = jnp.maximum(z, n - 1 - z)
 
     def arrive(distance, _):
-        for side in range(2):
-            source = z - distance if side == 0 else z + distance
-            inside = jnp.logical_and(source >= 0, source < n)
-
-            @pl.when(jnp.logical_and(inside, distance > 0))
-            def _():
-                for part in range(2):
+        for part in range(2):
+            for side in range(2):
+                source = z - distance if side == 0 else z + distance
+                inside = jnp.logical_and(source >= 0, source < n)
+
+                @pl.when(jnp.logical_and(inside, distance > 0))
+                def _():
                     row_copy(source, part, side).wait_recv()
                     send_on(source, part)
+
+        @pl.when(jnp.logical_and(beside, distance == 1))
+        def _():
+            down_copy(0).wait_recv()
+            y_copy(0).start()
+            x_copy(0, 0, True).start()
+
+        @pl.when(jnp.logical_and(beside, distance == 2))
+        def _():
+            y_taken(0).wait_recv()
+            x_copy(1, 0, True).start()
+            down_copy(1).wait_recv()
+            y_copy(1).start()
+            x_copy(0, 1, True).start()
+
+        @pl.when(jnp.logical_and(beside, distance == 3))
+        def _():
+            y_taken(1).wait_recv()
+            x_copy(1, 1, True).start()
+            for j in range(2):
+                core_copy(j, True).start()
 
         def one(side, _):
             source = z - distance + 2 * distance * side
@@ -510,7 +598,7 @@
 
             @pl.when(jnp.logical_and(inside, jnp.logical_or(distance > 0, side == 0)))
             def _():
-                project(source, jnp.where(distance == farthest, gate_tile, 2 * gate_tile))
+                project(source)
 
             return 0
 
@@ -519,13 +607,9 @@
 
     lax.fori_loop(0, n, arrive, 0)
 
-    def late_gate(side, _):
-        source = z - farthest + 2 * farthest * side
-
-        @pl.when(jnp.logical_and(source >= 0, source < n))
-        def _():
-            project_tiles(source, gate_tile, 2 * gate_tile)
-
+    def gate_tiles(i, _):
+        columns = pl.ds(pl.multiple_of(inner + i * 256, 256), 256)
+        proj[pl.ds(PAD, total), columns] = bdot(rows_all[...], wide[:, columns]).astype(jnp.bfloat16)
         return 0
 
     each_other(lambda i: out_copy(z, i).start())
@@ -652,9 +736,18 @@
                     ).astype(jnp.bfloat16)
                 end_copy(c).start()
 
-    lax.fori_loop(0, 2, late_gate, 0)
+    lax.fori_loop(0, gate_tile // 2, gate_tiles, 0)
     for c in range(quads):
         hand_on(c, s == 1)
+    lax.fori_loop(gate_tile // 2, gate_tile, gate_tiles, 0)
+
+    @pl.when(beside)
+    def _():
+        for k in range(2):
+            for c in range(2):
+                x_copy(k, c, False).wait_recv()
+            core_copy(2 + k, True).start()
+
     lax.fori_loop(0, n, take_out, 0)
 
     scores = [
@@ -701,6 +794,25 @@
         )
     squares[z] = local
     each_other(lambda i: square_copy(z, i).start())
+
+    def mix_copy(target):
+        place = pl.ds(pl.multiple_of(target * rows, rows), rows)
+        return remote(
+            pre.at[place, :],
+            far.at[place, :],
+            m_send.at[target],
+            m_recv.at[target],
+            {"tp": jnp.where(z == 0, 1, n - 2)},
+        )
+
+    @pl.when(at_end)
+    def _():
+        for q in range(pairs):
+            columns = slice(q * LANES, (q + 1) * LANES)
+            pre[:, columns] = (acc[:, columns] * norm_gain[:, columns]).astype(jnp.bfloat16)
+        for i in range(n - 1):
+            mix_copy(jnp.where(z == 0, n - 1 - i, i)).start()
+
     loads[4].wait()
     each_other(lambda i: square_copy(i, z).wait_recv())
     sum_all = squares[0]
@@ -708,6 +820,7 @@
         sum_all = sum_all + squares[i]
     inverse = lax.rsqrt(sum_all / (n * heads // GROUPS * HEAD_DIM) + epsilon)
     inverse = jnp.concatenate([inverse] * (LANES // 8), axis=0).T
+    run_ref[...] = inverse
     for q in range(pairs):
         columns = slice(q * LANES, (q + 1) * LANES)
         g = (2 * q) % GROUPS
@@ -733,6 +846,25 @@
             receive.at[target, p],
             {"tp": z + way},
         )
+
+    def far_partial(target, p):
+        place = pl.ds(pl.multiple_of(target * rows, rows), rows)
+        return bdot(far[place, :], spare[:, p])
+
+    def take_far(target):
+        place = pl.ds(pl.multiple_of(target * rows, rows), rows)
+        mix_copy(target).wait_recv()
+        scale = run_ref[place, :]
+        for q in range(pairs):
+            columns = slice(q * LANES, (q + 1) * LANES)
+            far[place, columns] = (
+                far[place, columns].astype(jnp.float32) * pair_of(scale, (2 * q) % GROUPS)
+            ).astype(jnp.bfloat16)
+
+    @pl.when(beside)
+    def _():
+        for j in range(4):
+            core_copy(j, False).wait_recv()
 
     items = (n - 1) * pieces
     lag = 3
@@ -747,11 +879,26 @@
             more = z < n - 1 if side == 0 else z > 0
             active = jnp.logical_and(active, jnp.logical_and(i >= 0, i < items))
 
+            has_far = z == n - 2 if side == 0 else z == 1
+            is_end = z == n - 1 if side == 0 else z == 0
+            use_far = jnp.logical_and(has_far, p < shared)
+            active = jnp.logical_and(active, jnp.logical_or(p >= shared, jnp.logical_not(is_end)))
+
+            @pl.when(jnp.logical_and(active, jnp.logical_and(has_far, p == 0)))
+            def _():
+                take_far(target)
+
             @pl.when(active)
             def _():
                 value = partial_of(target, columns_of(p))
 
-                @pl.when(more)
+                @pl.when(use_far)
+                def _():
+                    stage[target, :, columns_of(p)] = (
+                        value + far_partial(target, columns_of(p))
+                    ).astype(jnp.bfloat16)
+
+                @pl.when(jnp.logical_and(more, jnp.logical_not(use_far)))
                 def _():
                     sum_copy(target, p, side).wait_recv()
                     stage[target, :, columns_of(p)] = (
@@ -764,10 +911,19 @@
 
                 sum_copy(target, p, side).start()
 
+        @pl.when(jnp.logical_and(beside, t == items))
+        def _():
+            take_far(z)
+
         @pl.when(jnp.logical_and(t >= items, t < items + pieces))
         def _():
             columns = columns_of(t - items)
-            own_sum[:, columns] = tokens[:, columns].astype(jnp.float32) + partial_of(z, columns)
+            own = tokens[:, columns].astype(jnp.float32) + partial_of(z, columns)
+            own_sum[:, columns] = own
+
+            @pl.when(jnp.logical_and(beside, t - items < shared))
+            def _():
+                own_sum[:, columns] = own + far_partial(z, columns)
 
         return 0
 
@@ -775,17 +931,19 @@
 
     def finish(p, _):
         columns = columns_of(p)
-        @pl.when(z < n - 1)
-        def _():
-            sum_copy(z, p, 0).wait_recv()
-
-        @pl.when(z > 0)
-        def _():
-            sum_copy(z, p, 1).wait_recv()
+        lands = (
+            jnp.logical_and(z < n - 1, jnp.logical_or(z != n - 2, p >= shared)),
+            jnp.logical_and(z > 0, jnp.logical_or(z != 1, p >= shared)),
+        )
+        for side in range(2):
+
+            @pl.when(lands[side])
+            def _():
+                sum_copy(z, p, side).wait_recv()
 
         none = jnp.zeros((rows, piece_w), jnp.float32)
-        right = jnp.where(z < n - 1, from_right[z, :, columns].astype(jnp.float32), none)
-        left = jnp.where(z > 0, from_left[z, :, columns].astype(jnp.float32), none)
+        right = jnp.where(lands[0], from_right[z, :, columns].astype(jnp.float32), none)
+        left = jnp.where(lands[1], from_left[z, :, columns].astype(jnp.float32), none)
         out[:, columns] = (own_sum[:, columns] + right + left).astype(jnp.bfloat16)
         return 0
 
@@ -817,7 +975,7 @@
             sum_copy(i, p, 0).wait_send()
             return 0
 
-        lax.fori_loop(0, pieces, sent_sum, 0)
+        lax.fori_loop(jnp.where(at_end, shared, 0), pieces, sent_sum, 0)
 
     each_other(sent_small)
 
@@ -828,6 +986,22 @@
             state_tail(z, other).wait_send()
         for c in range(quads):
             end_copy(c).wait_send()
+
+    @pl.when(at_end)
+    def _():
+        for c in range(2):
+            down_copy(c).wait_send()
+        for i in range(n - 1):
+            mix_copy(jnp.where(z == 0, n - 1 - i, i)).wait_send()
+
+    @pl.when(beside)
+    def _():
+        for c in range(2):
+            y_copy(c).wait_send()
+            for k in range(2):
+                x_copy(k, c, True).wait_send()
+        for j in range(4):
+            core_copy(j, True).wait_send()
 
 
 def body(
@@ -852,13 +1026,13 @@
     total = n * rows
     all_states = n * state_w
     quads = heads // GROUPS
-    pieces = 8
+    pieces, shared = 8, 4
     bf16, f32 = jnp.bfloat16, jnp.float32
     vmem = pl.BlockSpec(memory_space=pltpu.VMEM)
     far = pl.BlockSpec(memory_space=pl.ANY)
     dma = pltpu.SemaphoreType.DMA
     return pl.pallas_call(
-        partial(fused_kernel, n, shards),
+        partial(fused_kernel, n, shards, shared),
         out_shape=jax.ShapeDtypeStruct((rows, width), bf16),
         in_specs=[far, vmem, far, far, far, far, vmem, vmem, vmem, vmem, vmem, vmem, far],
         out_specs=vmem,
@@ -885,6 +1059,9 @@
             pltpu.VMEM((n, rows, width), bf16),
             pltpu.VMEM((n, rows, width), bf16),
             pltpu.VMEM((rows, width), f32),
+            pltpu.VMEM((inner, width // pieces * shared), bf16),
+            pltpu.VMEM((total, inner), bf16),
+            pltpu.VMEM((total, inner), bf16),
             dma((6,)),
             pltpu.SemaphoreType.REGULAR((2,)),
             pltpu.SemaphoreType.REGULAR,
@@ -907,6 +1084,16 @@
             dma((n, pieces)),
             dma((n, pieces)),
             dma((n, pieces)),
+            dma((2,)),
+            dma((2,)),
+            dma((2,)),
+            dma((2,)),
+            dma((2, 2)),
+            dma((2, 2)),
+            dma((4,)),
+            dma((4,)),
+            dma((n,)),
+            dma((n,)),
         ],
         compiler_params=pltpu.CompilerParams(
             collective_id=0, has_side_effects=True, vmem_limit_bytes=62 * 1024 * 1024
@@ -937,7 +1124,10 @@
         rows = tokens.shape[0] // (mesh.shape["dp"] * shards * n)
         heads, state_w = proj_step.shape[1] // n, proj_states.shape[1] // n
         fits = (
-            rows % 32 == 0
+            n == 4
+            and shards == 4
+            and mesh.shape["dp"] == 2
+            and rows % 32 == 0
             and (rows * n) % BLOCK == 0
             and state_w == 2 * STATE
             and heads % GROUPS == 0

time: 105 us -> 95.5 us (0.910)
  Pallas kernels: 103 us -> 93 us
    pallas_call x1, Pallas kernels: 103 us -> 93 us  [body(): pl.pallas_call(partial(fused_kernel, n, shards, shared), out_shape=jax.Sh...]
where the time goes in v2:
time: 95.5 us; the launch traced here: 94.9 us
  Pallas kernels  93 us (97%)
  local copies, waits for them, and re-layouts  1.87 us (2%)
    pallas_call x1, Pallas kernels, body(): pl.pallas_call(partial(fused_kernel, n, shards, shared), out_shape=jax.Sh...  93 us

profile of v2, /device:TPU:10, one launch (start us, length us, event | category | flops | bytes accessed | tf_op | source)
XLA Modules:
  0.0 94.9 jit_solution(63052825551155108)
XLA Ops:
  0.0 93.0 %shard_map.127 = bf16[64,4096]{1,0:T(8,128)(2,1)} custom-call(bf16[64,4096]{1,0:T(8,128)(2,1)} %tokens_far.1, f32[1,4096]{1,0:T(1,128)} %bitcast.7, bf16[4096,1024]{1,0:T(8,128)(2,1)} %w_inner.1, bf16[4096,1024]{1,0:T(8,128)(2,1)} %w_gate.1, bf16[4096,256]{1,0:T(8,128)(2,1)} %w_states.1, bf16[16,4096]{1,0:T(8,128)(2,1)} %bitcast.6, f32[1,16]{1,0:T(1,128)} %bitcast.9, ...), custom_call_target="tpu_custom_call" | custom-call | tf_op jit(solution)/shard_map/pallas_call | solution.py:1034
  93.0 1.9 %copy.15 = bf16[64,4096]{1,0:T(8,128)(2,1)} copy(bf16[64,4096]{1,0:T(8,128)(2,1)} %shard_map.127) | data formatting | bytes 1048576

commit v3 on v2

--- a/solution.py
+++ b/solution.py
@@ -235,20 +235,26 @@
     shards,
     shared,
     tokens_far,
-    pre_gain,
+    pre_gain_far,
     w_inner,
     w_gate,
     w_states,
     w_step,
+    step_bias_far,
+    log_rate_far,
+    taps_inner_far,
+    taps_states,
+    skip_gain_far,
+    norm_gain_far,
+    w_out,
+    out,
+    tokens,
+    pre_gain,
     step_bias,
     log_rate,
     taps_inner,
-    taps_states,
     skip_gain,
     norm_gain,
-    w_out,
-    out,
-    tokens,
     wide,
     step_w,
     wout,
@@ -273,7 +279,9 @@
     spare,
     pre,
     far,
+    done,
     load_sem,
+    o_sem,
     line,
     ahead,
     g_send,
@@ -320,8 +328,23 @@
     across = lax.rem(s + shards // 2, shards)
     sibling = s + 1 - 2 * lax.rem(s, 2)
 
-    token_load = pltpu.make_async_copy(tokens_far, tokens, load_sem.at[5])
-    token_load.start()
+    early = [
+        pltpu.make_async_copy(source, target, load_sem.at[5 + i])
+        for i, (source, target) in enumerate(
+            (
+                (tokens_far, tokens),
+                (pre_gain_far, pre_gain),
+                (taps_states, taps_all.at[z]),
+                (step_bias_far, step_bias),
+                (log_rate_far, log_rate),
+                (taps_inner_far, taps_inner),
+                (skip_gain_far, skip_gain),
+                (norm_gain_far, norm_gain),
+            )
+        )
+    ]
+    for load in early:
+        load.start()
     barrier = pltpu.get_barrier_semaphore()
     neighbours = (
         (z > 0, {"tp": z - 1}),
@@ -346,7 +369,8 @@
         pltpu.make_async_copy(w_gate, wide.at[:, pl.ds(inner, inner)], load_sem.at[3]),
         pltpu.make_async_copy(w_out, wout, load_sem.at[4]),
     ]
-    token_load.wait()
+    for load in early[:2]:
+        load.wait()
     for load in loads[:4]:
         load.start()
 
@@ -358,8 +382,7 @@
         rows_all[place, :] = (value * scale * pre_gain[...]).astype(jnp.bfloat16)
         return 0
 
-    lax.fori_loop(0, half // 16, own_rows, 0)
-    taps_all[z] = taps_states[...]
+    lax.fori_loop(half // 16, rows // 16, own_rows, 0)
 
     @pl.when(s == 0)
     def _():
@@ -429,10 +452,10 @@
         def _():
             down_copy(c).start()
 
+    send_on(z, 1)
+    send_down(0)
+    lax.fori_loop(0, half // 16, own_rows, 0)
     send_on(z, 0)
-    send_down(0)
-    lax.fori_loop(half // 16, rows // 16, own_rows, 0)
-    send_on(z, 1)
     send_down(1)
 
     def greet_line(side, condition):
@@ -475,6 +498,9 @@
             block, block, s_send.at[chunk, other], s_recv.at[source, chunk], {"tp": other}
         )
 
+    def is_edge(i):
+        return jnp.logical_or(i == 0, i == n - 1)
+
     def out_copy(source, other):
         block = states.at[
             pl.ds(PAD, total), pl.ds(pl.multiple_of(source * state_w + STATE, LANES), STATE)
@@ -496,6 +522,8 @@
 
         lax.fori_loop(0, n, one, 0)
 
+    for load in early[2:]:
+        load.wait()
     each_other(lambda i: tap_copy(z, i).start())
 
     def inner_tail():
@@ -523,45 +551,61 @@
 
     gate_tile = inner // 256
 
-    def project_tiles(chunk, first, end):
-        piece = pl.ds(pl.multiple_of(chunk * rows, rows), rows)
-        place = pl.ds(pl.multiple_of(PAD + chunk * rows, 16), rows)
+    def project(start, size):
+        piece = pl.ds(pl.multiple_of(start, size), size)
+        place = pl.ds(pl.multiple_of(PAD + start, 16), size)
+        own = pl.ds(pl.multiple_of(z * state_w, LANES), state_w)
+        tail = jnp.logical_and(start + size == total, s < shards - 1)
+        states[place, own] = bdot(
+            rows_all[piece, :], wide[:, 2 * inner : 2 * inner + state_w]
+        ).astype(jnp.bfloat16)
+
+        @pl.when(tail)
+        def _():
+            pl.semaphore_wait(ahead, 1)
+            for other in range(n):
+                state_tail(z, other).start()
+
+        if size == rows:
+            send_in(start // rows)
+        else:
+
+            @pl.when(lax.rem(start, rows) == 0)
+            def _():
+                send_in(start // rows)
+                each_other(lambda i: out_copy(z, i).start())
+
+        raw_step[piece, :] = lax.dot_general(
+            rows_all[piece, :], step_w[...], NT, preferred_element_type=jnp.float32
+        )
 
         def tile(i, _):
             columns = pl.ds(pl.multiple_of(i * 256, 256), 256)
             proj[place, columns] = bdot(rows_all[piece, :], wide[:, columns]).astype(jnp.bfloat16)
             return 0
 
-        lax.fori_loop(first, end, tile, 0)
-
-    def project(chunk):
-        piece = pl.ds(pl.multiple_of(chunk * rows, rows), rows)
-        place = pl.ds(pl.multiple_of(PAD + chunk * rows, 16), rows)
-        own = pl.ds(pl.multiple_of(z * state_w, LANES), state_w)
-        states[place, own] = bdot(
-            rows_all[piece, :], wide[:, 2 * inner : 2 * inner + state_w]
-        ).astype(jnp.bfloat16)
+        lax.fori_loop(0, gate_tile, tile, 0)
+
+        @pl.when(tail)
+        def _():
+            inner_tail().start()
+
+    def gate_rows(start, size):
+        piece = pl.ds(pl.multiple_of(start, rows), size)
+        place = pl.ds(pl.multiple_of(PAD + start, 16), size)
+
+        def tile(i, _):
+            columns = pl.ds(pl.multiple_of(inner + i * 256, 256), 256)
+            proj[place, columns] = bdot(rows_all[piece, :], wide[:, columns]).astype(jnp.bfloat16)
+            return 0
+
+        lax.fori_loop(0, gate_tile, tile, 0)
+
+    def send_in(chunk):
         each_other(lambda i: in_copy(z, chunk, i).start())
 
-        @pl.when(jnp.logical_and(chunk == n - 1, s < shards - 1))
-        def _():
-            pl.semaphore_wait(ahead, 1)
-            for other in range(n):
-                state_tail(z, other).start()
-
-        raw_step[piece, :] = lax.dot_general(
-            rows_all[piece, :], step_w[...], NT, preferred_element_type=jnp.float32
-        )
-
-        project_tiles(chunk, 0, gate_tile)
-
-        @pl.when(jnp.logical_and(chunk == n - 1, s < shards - 1))
-        def _():
-            inner_tail().start()
-
-
     def arrive(distance, _):
-        for part in range(2):
+        for part in (1, 0):
             for side in range(2):
                 source = z - distance if side == 0 else z + distance
                 inside = jnp.logical_and(source >= 0, source < n)
@@ -585,34 +629,49 @@
             y_copy(1).start()
             x_copy(0, 1, True).start()
 
-        @pl.when(jnp.logical_and(beside, distance == 3))
-        def _():
-            y_taken(1).wait_recv()
-            x_copy(1, 1, True).start()
-            for j in range(2):
-                core_copy(j, True).start()
-
         def one(side, _):
             source = z - distance + 2 * distance * side
             inside = jnp.logical_and(source >= 0, source < n)
 
             @pl.when(jnp.logical_and(inside, jnp.logical_or(distance > 0, side == 0)))
             def _():
-                project(source)
+                project(source * rows, rows)
 
             return 0
 
         lax.fori_loop(0, 2, one, 0)
         return 0
 
-    lax.fori_loop(0, n, arrive, 0)
-
-    def gate_tiles(i, _):
-        columns = pl.ds(pl.multiple_of(inner + i * 256, 256), 256)
-        proj[pl.ds(PAD, total), columns] = bdot(rows_all[...], wide[:, columns]).astype(jnp.bfloat16)
-        return 0
-
-    each_other(lambda i: out_copy(z, i).start())
+    lax.fori_loop(0, n - 1, arrive, 0)
+
+    @pl.when(beside)
+    def _():
+        y_taken(1).wait_recv()
+        x_copy(1, 1, True).start()
+        for j in range(2):
+            core_copy(j, True).start()
+
+    @pl.when(jnp.logical_not(at_end))
+    def _():
+        each_other(lambda i: out_copy(z, i).start())
+        gate_rows(0, total)
+
+    @pl.when(at_end)
+    def _():
+        gate_rows(jnp.where(z == 0, 0, rows), total - rows)
+
+        def last_half(i, _):
+            part = 1 - i
+            for side in range(2):
+
+                @pl.when(z == (n - 1 if side == 0 else 0))
+                def _():
+                    row_copy(n - 1 - z, part, side).wait_recv()
+
+            project((n - 1 - z) * rows + part * half, half)
+            return 0
+
+        lax.fori_loop(0, 2, last_half, 0)
 
     step = raw_step[...] + step_bias[...]
     step = jnp.maximum(step, 0.0) + jnp.log1p(jnp.exp(-jnp.abs(step)))
@@ -736,10 +795,13 @@
                     ).astype(jnp.bfloat16)
                 end_copy(c).start()
 
-    lax.fori_loop(0, gate_tile // 2, gate_tiles, 0)
     for c in range(quads):
         hand_on(c, s == 1)
-    lax.fori_loop(gate_tile // 2, gate_tile, gate_tiles, 0)
+
+    @pl.when(at_end)
+    def _():
+        gate_rows((n - 1 - z) * rows, rows)
+
 
     @pl.when(beside)
     def _():
@@ -770,12 +832,14 @@
                 weights = (scores[k % GROUPS][low_t:high_t, :high_t] * table).astype(jnp.bfloat16)
                 both.append(bdot(weights, stepped[:high_t, :]))
             acc[low_t:high_t, columns] = jnp.where(low, both[0], both[1]) + direct[low_t:high_t, :]
+        if q % per_quad == per_quad - 1:
+            hand_on(q // per_quad, s == 2)
     sums = [jnp.zeros((total, LANES), jnp.float32) for _ in range(per_quad)]
     for q in range(pairs):
         columns = slice(q * LANES, (q + 1) * LANES)
         h = 2 * q
         if q % per_quad == 0:
-            hand_on(q // per_quad, s > 1)
+            hand_on(q // per_quad, s > 2)
         came = state_in[:, columns]
         carried = jnp.where(
             low, bdot(group_out(h % GROUPS), came), bdot(group_out((h + 1) % GROUPS), came)
@@ -821,12 +885,14 @@
     inverse = lax.rsqrt(sum_all / (n * heads // GROUPS * HEAD_DIM) + epsilon)
     inverse = jnp.concatenate([inverse] * (LANES // 8), axis=0).T
     run_ref[...] = inverse
-    for q in range(pairs):
-        columns = slice(q * LANES, (q + 1) * LANES)
-        g = (2 * q) % GROUPS
-        mixed[:, columns] = (
-            acc[:, columns] * pair_of(inverse, g) * norm_gain[:, columns]
-        ).astype(jnp.bfloat16)
+    def mix(target):
+        place = pl.ds(pl.multiple_of(target * rows, rows), rows)
+        scale = run_ref[place, :]
+        for q in range(pairs):
+            columns = slice(q * LANES, (q + 1) * LANES)
+            mixed[place, columns] = (
+                acc[place, columns] * pair_of(scale, (2 * q) % GROUPS) * norm_gain[:, columns]
+            ).astype(jnp.bfloat16)
 
     pieces = r_send.shape[1]
     piece_w = width // pieces
@@ -840,8 +906,8 @@
     def sum_copy(target, p, side):
         landing, receive, way = (from_right, rl_recv, -1) if side == 0 else (from_left, rr_recv, 1)
         return remote(
-            stage.at[target, :, columns_of(p)],
-            landing.at[target, :, columns_of(p)],
+            stage.at[target, p],
+            landing.at[target, p],
             r_send.at[target, p],
             receive.at[target, p],
             {"tp": z + way},
@@ -884,9 +950,13 @@
             use_far = jnp.logical_and(has_far, p < shared)
             active = jnp.logical_and(active, jnp.logical_or(p >= shared, jnp.logical_not(is_end)))
 
-            @pl.when(jnp.logical_and(active, jnp.logical_and(has_far, p == 0)))
+            @pl.when(jnp.logical_and(active, p == jnp.where(is_end, shared, 0)))
             def _():
-                take_far(target)
+                mix(target)
+
+                @pl.when(has_far)
+                def _():
+                    take_far(target)
 
             @pl.when(active)
             def _():
@@ -894,26 +964,30 @@
 
                 @pl.when(use_far)
                 def _():
-                    stage[target, :, columns_of(p)] = (
+                    stage[target, p] = (
                         value + far_partial(target, columns_of(p))
                     ).astype(jnp.bfloat16)
 
                 @pl.when(jnp.logical_and(more, jnp.logical_not(use_far)))
                 def _():
                     sum_copy(target, p, side).wait_recv()
-                    stage[target, :, columns_of(p)] = (
-                        value + landing[target, :, columns_of(p)].astype(jnp.float32)
+                    stage[target, p] = (
+                        value + landing[target, p].astype(jnp.float32)
                     ).astype(jnp.bfloat16)
 
                 @pl.when(jnp.logical_not(more))
                 def _():
-                    stage[target, :, columns_of(p)] = value.astype(jnp.bfloat16)
+                    stage[target, p] = value.astype(jnp.bfloat16)
 
                 sum_copy(target, p, side).start()
 
-        @pl.when(jnp.logical_and(beside, t == items))
-        def _():
-            take_far(z)
+        @pl.when(t == items)
+        def _():
+            mix(z)
+
+            @pl.when(beside)
+            def _():
+                take_far(z)
 
         @pl.when(jnp.logical_and(t >= items, t < items + pieces))
         def _():
@@ -942,10 +1016,15 @@
                 sum_copy(z, p, side).wait_recv()
 
         none = jnp.zeros((rows, piece_w), jnp.float32)
-        right = jnp.where(lands[0], from_right[z, :, columns].astype(jnp.float32), none)
-        left = jnp.where(lands[1], from_left[z, :, columns].astype(jnp.float32), none)
-        out[:, columns] = (own_sum[:, columns] + right + left).astype(jnp.bfloat16)
+        right = jnp.where(lands[0], from_right[z, p].astype(jnp.float32), none)
+        left = jnp.where(lands[1], from_left[z, p].astype(jnp.float32), none)
+        done[:, columns] = (own_sum[:, columns] + right + left).astype(jnp.bfloat16)
+        out_store(p).start()
         return 0
+
+    def out_store(p):
+        columns = columns_of(p)
+        return pltpu.make_async_copy(done.at[:, columns], out.at[:, columns], o_sem.at[p])
 
     lax.fori_loop(0, pieces, finish, 0)
 
@@ -978,6 +1057,12 @@
         lax.fori_loop(jnp.where(at_end, shared, 0), pieces, sent_sum, 0)
 
     each_other(sent_small)
+
+    def stored(p, _):
+        out_store(p).wait()
+        return 0
+
+    lax.fori_loop(0, pieces, stored, 0)
 
     @pl.when(s < shards - 1)
     def _():
@@ -1028,16 +1113,21 @@
     quads = heads // GROUPS
     pieces, shared = 8, 4
     bf16, f32 = jnp.bfloat16, jnp.float32
-    vmem = pl.BlockSpec(memory_space=pltpu.VMEM)
     far = pl.BlockSpec(memory_space=pl.ANY)
     dma = pltpu.SemaphoreType.DMA
     return pl.pallas_call(
         partial(fused_kernel, n, shards, shared),
         out_shape=jax.ShapeDtypeStruct((rows, width), bf16),
-        in_specs=[far, vmem, far, far, far, far, vmem, vmem, vmem, vmem, vmem, vmem, far],
-        out_specs=vmem,
+        in_specs=[far] * 13,
+        out_specs=far,
         scratch_shapes=[
             pltpu.VMEM((rows, width), bf16),
+            pltpu.VMEM((1, width), f32),
+            pltpu.VMEM((1, heads), f32),
+            pltpu.VMEM((1, heads), f32),
+            pltpu.VMEM(conv_inner.shape, f32),
+            pltpu.VMEM((1, heads), f32),
+            pltpu.VMEM((1, inner), f32),
             pltpu.VMEM((width, 2 * inner + state_w), bf16),
             pltpu.VMEM((heads, width), bf16),
             pltpu.VMEM((inner, width), bf16),
@@ -1055,14 +1145,16 @@
             pltpu.VMEM((STATE, inner), bf16),
             pltpu.VMEM((n, 8, total), f32),
             pltpu.VMEM((total, inner), bf16),
-            pltpu.VMEM((n, rows, width), bf16),
-            pltpu.VMEM((n, rows, width), bf16),
-            pltpu.VMEM((n, rows, width), bf16),
+            pltpu.VMEM((n, pieces, rows, width // pieces), bf16),
+            pltpu.VMEM((n, pieces, rows, width // pieces), bf16),
+            pltpu.VMEM((n, pieces, rows, width // pieces), bf16),
             pltpu.VMEM((rows, width), f32),
             pltpu.VMEM((inner, width // pieces * shared), bf16),
             pltpu.VMEM((total, inner), bf16),
             pltpu.VMEM((total, inner), bf16),
-            dma((6,)),
+            pltpu.VMEM((rows, width), bf16),
+            dma((13,)),
+            dma((pieces,)),
             pltpu.SemaphoreType.REGULAR((2,)),
             pltpu.SemaphoreType.REGULAR,
             dma((2, n, 2)),

time: 95.5 us -> 94 us (0.984)
  Pallas kernels: 93 us -> 91.5 us
    pallas_call x1, Pallas kernels: 93 us -> 91.5 us  [body(): pl.pallas_call(partial(fused_kernel, n, shards, shared), out_shape=jax.Sh...]
where the time goes in v3:
time: 94 us; the launch traced here: 93.4 us
  Pallas kernels  91.5 us (97%)
  local copies, waits for them, and re-layouts  1.87 us (2%)
    pallas_call x1, Pallas kernels, body(): pl.pallas_call(partial(fused_kernel, n, shards, shared), out_shape=jax.Sh...  91.5 us

profile of v3, /device:TPU:10, one launch (start us, length us, event | category | flops | bytes accessed | tf_op | source)
XLA Modules:
  0.0 93.4 jit_solution(1718240964707074942)
XLA Ops:
  0.0 91.5 %shard_map.127 = bf16[64,4096]{1,0:T(8,128)(2,1)} custom-call(bf16[64,4096]{1,0:T(8,128)(2,1)} %tokens_far.1, f32[1,4096]{1,0:T(1,128)} %bitcast.7, bf16[4096,1024]{1,0:T(8,128)(2,1)} %w_inner.1, bf16[4096,1024]{1,0:T(8,128)(2,1)} %w_gate.1, bf16[4096,256]{1,0:T(8,128)(2,1)} %w_states.1, bf16[16,4096]{1,0:T(8,128)(2,1)} %bitcast.6, f32[1,16]{1,0:T(1,128)} %bitcast.9, ...), custom_call_target="tpu_custom_call" | custom-call | tf_op jit(solution)/shard_map/pallas_call | solution.py:1118
  91.5 1.9 %copy.15 = bf16[64,4096]{1,0:T(8,128)(2,1)} copy(bf16[64,4096]{1,0:T(8,128)(2,1)} %shard_map.127) | data formatting | bytes 1048576

commit v4 on v3

--- a/solution.py
+++ b/solution.py
@@ -678,8 +678,12 @@
     decay = -jnp.exp(log_rate[...]) * step
     place_t = lax.broadcasted_iota(jnp.int32, (total, total), 0)
     place_s = lax.broadcasted_iota(jnp.int32, (total, total), 1)
-    tri = (place_t >= place_s).astype(jnp.float32)
-    run = jnp.dot(tri, decay, precision=highest, preferred_element_type=jnp.float32)
+    tri = (place_t >= place_s).astype(jnp.bfloat16)
+    decay_high = decay.astype(jnp.bfloat16)
+    rest = decay - decay_high.astype(jnp.float32)
+    decay_mid = rest.astype(jnp.bfloat16)
+    decay_low = (rest - decay_mid.astype(jnp.float32)).astype(jnp.bfloat16)
+    run = bdot(tri, decay_high) + (bdot(tri, decay_mid) + bdot(tri, decay_low))
     run_ref[...] = jnp.zeros(run_ref.shape, jnp.float32)
     run_ref[:, 0:heads] = run
     run_t = run_ref[...].T
@@ -810,6 +814,8 @@
                 x_copy(k, c, False).wait_recv()
             core_copy(2 + k, True).start()
 
+    for c in range(quads):
+        hand_on(c, s == 2)
     lax.fori_loop(0, n, take_out, 0)
 
     scores = [
@@ -832,8 +838,6 @@
                 weights = (scores[k % GROUPS][low_t:high_t, :high_t] * table).astype(jnp.bfloat16)
                 both.append(bdot(weights, stepped[:high_t, :]))
             acc[low_t:high_t, columns] = jnp.where(low, both[0], both[1]) + direct[low_t:high_t, :]
-        if q % per_quad == per_quad - 1:
-            hand_on(q // per_quad, s == 2)
     sums = [jnp.zeros((total, LANES), jnp.float32) for _ in range(per_quad)]
     for q in range(pairs):
         columns = slice(q * LANES, (q + 1) * LANES)

time: 94 us -> 93.2 us (level)
  no operation moved by 1% of the time
where the time goes in v4:
time: 93.2 us; the launch traced here: 93 us
  Pallas kernels  91.2 us (98%)
  local copies, waits for them, and re-layouts  1.87 us (2%)
    pallas_call x1, Pallas kernels, body(): pl.pallas_call(partial(fused_kernel, n, shards, shared), out_shape=jax.Sh...  91.2 us
    unnamed x1, local copies, waits for them, and re-layouts  1.87 us

profile of v4, /device:TPU:10, one launch (start us, length us, event | category | flops | bytes accessed | tf_op | source)
XLA Modules:
  0.0 93.0 jit_solution(1556212710703816145)
XLA Ops:
  0.0 91.2 %shard_map.127 = bf16[64,4096]{1,0:T(8,128)(2,1)} custom-call(bf16[64,4096]{1,0:T(8,128)(2,1)} %tokens_far.1, f32[1,4096]{1,0:T(1,128)} %bitcast.7, bf16[4096,1024]{1,0:T(8,128)(2,1)} %w_inner.1, bf16[4096,1024]{1,0:T(8,128)(2,1)} %w_gate.1, bf16[4096,256]{1,0:T(8,128)(2,1)} %w_states.1, bf16[16,4096]{1,0:T(8,128)(2,1)} %bitcast.6, f32[1,16]{1,0:T(1,128)} %bitcast.9, ...), custom_call_target="tpu_custom_call" | custom-call | tf_op jit(solution)/shard_map/pallas_call | solution.py:1122
  91.2 1.9 %copy.15 = bf16[64,4096]{1,0:T(8,128)(2,1)} copy(bf16[64,4096]{1,0:T(8,128)(2,1)} %shard_map.127) | data formatting | bytes 1048576

commit v5 on v4

--- a/solution.py
+++ b/solution.py
@@ -767,14 +767,15 @@
             {"seq": s + 1, "tp": z},
         )
 
-    turned = [group_in(g).T for g in range(GROUPS)]
+    turned = [
+        jnp.concatenate((group_in(g).T, group_in(g + 1).T), axis=0) for g in range(0, GROUPS, 2)
+    ]
     for q in range(pairs):
         columns = slice(q * LANES, (q + 1) * LANES)
         h = 2 * q
         scaled = (x_mix[:, columns].astype(jnp.float32) * pair_of(reach, h)).astype(jnp.bfloat16)
-        ends[:, columns] = jnp.where(
-            low, bdot(turned[h % GROUPS], scaled), bdot(turned[(h + 1) % GROUPS], scaled)
-        )
+        both = bdot(turned[h % GROUPS // 2], scaled)
+        ends[:, columns] = jnp.where(low, both[:STATE], both[STATE:])
         if q % per_quad == per_quad - 1:
             c = q // per_quad
 
@@ -806,13 +807,6 @@
     def _():
         gate_rows((n - 1 - z) * rows, rows)
 
-
-    @pl.when(beside)
-    def _():
-        for k in range(2):
-            for c in range(2):
-                x_copy(k, c, False).wait_recv()
-            core_copy(2 + k, True).start()
 
     for c in range(quads):
         hand_on(c, s == 2)
@@ -838,6 +832,13 @@
                 weights = (scores[k % GROUPS][low_t:high_t, :high_t] * table).astype(jnp.bfloat16)
                 both.append(bdot(weights, stepped[:high_t, :]))
             acc[low_t:high_t, columns] = jnp.where(low, both[0], both[1]) + direct[low_t:high_t, :]
+    @pl.when(beside)
+    def _():
+        for k in range(2):
+            for c in range(2):
+                x_copy(k, c, False).wait_recv()
+            core_copy(2 + k, True).start()
+
     sums = [jnp.zeros((total, LANES), jnp.float32) for _ in range(per_quad)]
     for q in range(pairs):
         columns = slice(q * LANES, (q + 1) * LANES)

time: 93.2 us -> 93.3 us (level)
  no operation moved by 1% of the time
where the time goes in v5:
time: 93.3 us; the launch traced here: 93.1 us
  Pallas kernels  91.2 us (98%)
  local copies, waits for them, and re-layouts  1.87 us (2%)
    pallas_call x1, Pallas kernels, body(): pl.pallas_call(partial(fused_kernel, n, shards, shared), out_shape=jax.Sh...  91.2 us
    unnamed x1, local copies, waits for them, and re-layouts  1.87 us

profile of v5, /device:TPU:10, one launch (start us, length us, event | category | flops | bytes accessed | tf_op | source)
XLA Modules:
  0.0 93.1 jit_solution(17491881223634847668)
XLA Ops:
  0.0 91.2 %shard_map.127 = bf16[64,4096]{1,0:T(8,128)(2,1)} custom-call(bf16[64,4096]{1,0:T(8,128)(2,1)} %tokens_far.1, f32[1,4096]{1,0:T(1,128)} %bitcast.7, bf16[4096,1024]{1,0:T(8,128)(2,1)} %w_inner.1, bf16[4096,1024]{1,0:T(8,128)(2,1)} %w_gate.1, bf16[4096,256]{1,0:T(8,128)(2,1)} %w_states.1, bf16[16,4096]{1,0:T(8,128)(2,1)} %bitcast.6, f32[1,16]{1,0:T(1,128)} %bitcast.9, ...), custom_call_target="tpu_custom_call" | custom-call | tf_op jit(solution)/shard_map/pallas_call | solution.py:1123
  91.2 1.9 %copy.15 = bf16[64,4096]{1,0:T(8,128)(2,1)} copy(bf16[64,4096]{1,0:T(8,128)(2,1)} %shard_map.127) | data formatting | bytes 1048576
